TPU v7x, 128 devices: a whole 4x4x4 slice. The times are simulated.
128 devices in a mesh: dp: 16 (over y_hi, z, core), tensor: 8 (over y_lo, x).
Axes of the slice: x: 4, y: 4 (y_hi: 2, y_lo: 2; y = y_hi * 2 + y_lo), z: 4, core: 2. Of those that a mesh axis runs over, the one named last changes fastest.
Arguments:
- saved_queries: bfloat16 [16384, 8192], P('dp', 'tensor'), may hold values from -200 to 200
- saved_keys: bfloat16 [16384, 1024], P('dp', 'tensor'), may hold values from -200 to 200
- saved_values: bfloat16 [16384, 1024], P('dp', 'tensor'), may hold values from -6 to 6
- out_grad: bfloat16 [16384, 8192], P(('dp', 'tensor')), may hold values from -2.5 to 2.5
- act_exponent: int32 [1], replicated, may hold values from -6 to 3
- grad_exponent: int32 [1], replicated, may hold values from -4 to 1
Outputs:
- grad_weight: float32 [8192, 8192], P('dp', 'tensor')
All inputs are finite; a program needn't handle non-finite values.
Results may differ from a plain program's by a relative error of at most 0.012.
Values may be sent and summed in bfloat16 or wider, within the bound.
A program may use at most 128 MiB of HBM per device.

v0:
```python
import jax
import jax.numpy as jnp
from jax import lax
from jax.sharding import PartitionSpec as P

HEAD_DIM = 128
SATURATION = 448.0


def quantize(values_in, exponent):
    factor = SATURATION * jnp.exp2(-exponent[0].astype(jnp.float32))
    return jnp.clip(values_in * factor, -SATURATION, SATURATION).astype(jnp.bfloat16)


def attend(query_rows, key_rows, value_rows):
    scores = jnp.dot(query_rows, key_rows.T, preferred_element_type=jnp.float32) * HEAD_DIM ** (
        -0.5
    )
    positions = jnp.arange(query_rows.shape[0], dtype=jnp.int32)
    causal = positions[None, :] <= positions[:, None]
    scores = jnp.where(causal, scores, jnp.float32(-1e30))
    row_max = jnp.max(scores, axis=1, keepdims=True)
    weights = jnp.exp(scores - row_max)
    probabilities = (weights / jnp.sum(weights, axis=1, keepdims=True)).astype(jnp.bfloat16)
    return jnp.dot(probabilities, value_rows, preferred_element_type=jnp.float32)


def on_device(saved_queries, saved_keys, saved_values, out_grad, act_exponent, grad_exponent):
    seq_len = saved_queries.shape[0]
    local_width = saved_queries.shape[1]
    heads_here = local_width // HEAD_DIM
    dequant = jnp.exp2((act_exponent[0] + grad_exponent[0]).astype(jnp.float32)) / (
        SATURATION * SATURATION
    )

    def one_head(head_index, scaled_rows):
        query_rows = lax.dynamic_slice_in_dim(saved_queries, head_index * HEAD_DIM, HEAD_DIM, 1)
        attended = attend(query_rows, saved_keys, saved_values)
        return lax.dynamic_update_slice_in_dim(
            scaled_rows, quantize(attended, act_exponent), head_index * HEAD_DIM, 1
        )

    act_scaled = lax.fori_loop(
        0, heads_here, one_head, jnp.zeros((seq_len, local_width), jnp.bfloat16)
    )
    grad_scaled = quantize(out_grad.astype(jnp.float32), grad_exponent)
    running = lax.dot_general(
        lax.all_gather(grad_scaled, "tensor", axis=0, tiled=True),
        act_scaled,
        (((0,), (0,)), ((), ())),
        preferred_element_type=jnp.float32,
    )
    grad_weight = lax.psum_scatter(
        (running * dequant).astype(jnp.bfloat16), "dp", scatter_dimension=0, tiled=True
    ).astype(jnp.float32)
    return grad_weight


def solution(mesh):
    in_specs = (
        P("dp", "tensor"),
        P("dp", "tensor"),
        P("dp", "tensor"),
        P(("dp", "tensor"), None),
        P(),
        P(),
    )
    out_specs = P("dp", "tensor")
    return jax.shard_map(
        on_device, mesh=mesh, in_specs=in_specs, out_specs=out_specs, check_vma=False
    )
```

profile of v0, /device:TPU:0, one launch (start us, length us, event | category | flops | bytes accessed | tf_op | source)
XLA Modules:
  0.0 367.2 jit_solution(14772406896722090747)
XLA Ops:
  6.5 0.0 all-gather.2.cloned.1.call-start
  7.2 0.0 copy-start
  7.2 0.0 copy-start.1
  7.3 3.5 clamp_convert_fusion
  10.7 0.0 all-gather.2.cloned.1.call-update
  10.8 0.0 reduce-scatter.2.cloned.1.call-start
  11.6 0.3 broadcast_in_dim.25
  11.8 0.0 copy-done
  11.8 0.0 copy-done.1
  11.8 25.3 %while.15 = (s32[]{:T(128)}, bf16[1024,1024]{1,0:T(8,128)(2,1)S(1)}, bf16[1024,1024]{1,0:T(8,128)(2,1)}, bf16[1024,128]{1,0:T(8,128)(2,1)S(1)}, bf16[1024,128]{1...) while((s32[]{:T(128)}, bf16[1024,1024]{1,0:T(8,128)(2,1)S(1)}, ...), condition=%wide.region_3.4_spmd, body=%wide.region_0.3_spmd.sunk | while | flops 552990720 | bytes 13652127 | solution.py:43
  11.9 1.7 fusion.23
  13.5 0.5 fusion.24
  14.1 0.9 fusion.25
  15.0 1.7 fusion.23
  16.7 0.5 fusion.24
  17.2 0.9 fusion.25
  18.2 1.7 fusion.23
  19.8 0.5 fusion.24
  20.4 0.9 fusion.25
  21.3 1.7 fusion.23
  23.0 0.5 fusion.24
  23.6 0.9 fusion.25
  24.5 1.7 fusion.23
  26.2 0.5 fusion.24
  26.7 0.9 fusion.25
  27.7 1.7 fusion.23
  29.3 0.5 fusion.24
  29.9 0.9 fusion.25
  30.8 1.7 fusion.23
  32.5 0.5 fusion.24
  33.0 0.9 fusion.25
  34.0 1.7 fusion.23
  35.7 0.5 fusion.24
  36.2 0.9 fusion.25
  37.1 146.7 %all-gather.2.cloned.1.call-done = bf16[1024,8192]{1,0:T(8,128)(2,1)} async-done(((bf16[128,8192]{1,0:T(8,128)(2,1)}), bf16[1024,8192]{1,0:T(8,128)(2,1)}) %all-gather.2.cloned.1.call-update) | async-done | bytes 16777232 | tf_op jit(solution)/shard_map/all_gather | solution.py:48
  183.9 27.4 %multiply_convert_fusion = bf16[8192,1024]{1,0:T(8,128)(2,1)} fusion(bf16[1024,8192]{1,0:T(8,128)(2,1)} %all-gather.2.cloned.1.call-done, bf16[1024,1024]{1,0:T(8,128)(2,1)S(1)} %get-tuple-element.158, f32[]{:T(128)} %bitcast.2), kind=kOutput, calls=%fused_computation.16 | convolution fusion | flops 17196646400 | bytes 35651588 | tf_op jit(solution)/shard_map/dot_general | solution.py:47
  211.3 0.0 reduce-scatter.2.cloned.1.call-update
  211.3 146.3 %reduce-scatter.2.cloned.1.call-done = bf16[512,1024]{1,0:T(8,128)(2,1)} async-done(((bf16[8192,1024]{1,0:T(8,128)(2,1)}), bf16[512,1024]{1,0:T(8,128)(2,1)}) %reduce-scatter.2.cloned.1.call-update) | async-done | bytes 1048592 | tf_op jit(solution)/shard_map/reduce_scatter | solution.py:53
  357.6 2.8 convert_element_type.54
Async XLA Ops:
  6.5 177.3 %all-gather.2.cloned.1.call-start = ((), (), s32[]{:S(2)}) async-start(), calls=%async_computation.1 | async-start | bytes 18874368 | tf_op jit(solution)/shard_map/all_gather | solution.py:48
  7.2 4.6 %copy-start = (bf16[1024,128]{1,0:T(8,128)(2,1)S(1)}, bf16[1024,128]{1,0:T(8,128)(2,1)}, u32[]{:S(2)}) copy-start(bf16[1024,128]{1,0:T(8,128)(2,1)} %param.9) | copy-start | bytes 786436
  7.2 4.6 %copy-start.1 = (bf16[1024,128]{1,0:T(8,128)(2,1)S(1)}, bf16[1024,128]{1,0:T(8,128)(2,1)}, u32[]{:S(2)}) copy-start(bf16[1024,128]{1,0:T(8,128)(2,1)} %param.10) | copy-start | bytes 786436
  10.8 346.8 %reduce-scatter.2.cloned.1.call-start = ((), (), s32[]{:S(2)}) async-start(), calls=%async_computation.2 | async-start | bytes 17825792 | tf_op jit(solution)/shard_map/reduce_scatter | solution.py:53
Sparse Core Ops, SparseCore 0:
  10.9 172.9 all-gather.1
  211.4 146.1 reduce-scatter.1
where the time goes:
time: 368 us; the launch traced here: 367 us
  waiting for transfers between devices  293 us (80%)
  matrix products  48.3 us (13%)
  between operations  14.9 us (4%)
  other arithmetic  10.5 us (3%)
    all_gather x1, waiting for transfers between devices, on_device(): lax.all_gather(grad_scaled, 'tensor', axis=0, tiled=True)  147 us
    reduce_scatter x1, waiting for transfers between devices, on_device(): lax.psum_scatter((running * dequant).astype(jnp.bfloat16), 'dp', scatter_...  146 us
    dot_general x1, matrix products, on_device(): lax.dot_general(lax.all_gather(grad_scaled, 'tensor', axis=0, tiled=True)...  27.4 us
    dot_general x8, matrix products, attend(): jnp.dot(query_rows, key_rows.T, preferred_element_type=jnp.float32)  13.4 us
    dot_general x8, matrix products, attend(): jnp.dot(probabilities, value_rows, preferred_element_type=jnp.float32)  7.5 us
  transfers between devices with their start and end apart: 2, of which 2 were waited for; matrix products, arithmetic and copies ran while one was open for 7% of the time, Pallas kernels for 0%

commit v1 on v0

--- a/solution.py
+++ b/solution.py
@@ -45,7 +45,10 @@
     )
     grad_scaled = quantize(out_grad.astype(jnp.float32), grad_exponent)
     running = lax.dot_general(
-        lax.all_gather(grad_scaled, "tensor", axis=0, tiled=True),
+        jnp.concatenate(
+            lax.all_to_all(jnp.stack([grad_scaled] * lax.axis_size("tensor")), "tensor", 0, 0),
+            axis=0,
+        ),
         act_scaled,
         (((0,), (0,)), ((), ())),
         preferred_element_type=jnp.float32,

time: 368 us -> 459 us (1.25)
  waiting for transfers between devices: 293 us -> 374 us
  local copies, waits for them, and re-layouts: 0.26 us -> 6.22 us
  starting transfers between devices: 0.04 us -> 5.92 us
    all_to_all x0 -> x1, waiting for transfers between devices: none -> 158 us  [on_device(): lax.all_to_all(jnp.stack([grad_scaled] * lax.axis_size('tensor')), 'tenso...]
    all_gather x1 -> x0, waiting for transfers between devices: 147 us -> none  [on_device(): lax.all_gather(grad_scaled, 'tensor', axis=0, tiled=True)]
    reduce_scatter x1, waiting for transfers between devices: 146 us -> 216 us  [on_device(): lax.psum_scatter((running * dequant).astype(jnp.bfloat16), 'dp', scatter_...]
    another operation x0 -> x1, local copies, waits for them, and re-layouts: none -> 5.96 us  [on_device(): jnp.stack([grad_scaled] * lax.axis_size('tensor'))]
    all_to_all x0 -> x1, starting transfers between devices: none -> 5.88 us  [on_device(): lax.all_to_all(jnp.stack([grad_scaled] * lax.axis_size('tensor')), 'tenso...]
  transfers between devices with their start and end apart: 2 -> 2, of which waited for: 2 -> 2; matrix products, arithmetic and copies ran while one was open for 7% -> 6% of each run, Pallas kernels for 0% -> 0%
where the time goes in v1:
time: 459 us
  waiting for transfers between devices  374 us (81%)
  matrix products  48.2 us (11%)
  between operations  14.9 us (3%)
  other arithmetic  9.09 us (2%)
  local copies, waits for them, and re-layouts  6.22 us (1%)
  starting transfers between devices  5.92 us (1%)
    reduce_scatter x1, waiting for transfers between devices, on_device(): lax.psum_scatter((running * dequant).astype(jnp.bfloat16), 'dp', scatter_...  216 us
    all_to_all x1, waiting for transfers between devices, on_device(): lax.all_to_all(jnp.stack([grad_scaled] * lax.axis_size('tensor')), 'tenso...  158 us
    dot_general x1, matrix products, on_device(): lax.dot_general(jnp.concatenate(lax.all_to_all(jnp.stack([grad_scaled] *...  27.4 us
    dot_general x8, matrix products, attend(): jnp.dot(query_rows, key_rows.T, preferred_element_type=jnp.float32)  13.4 us
  transfers between devices with their start and end apart: 2, of which 2 were waited for; matrix products, arithmetic and copies ran while one was open for 6% of the time, Pallas kernels for 0%

profile of v1, /device:TPU:0, one launch (start us, length us, event | category | flops | bytes accessed | tf_op | source)
XLA Modules:
  0.0 458.8 jit_solution(8610701257877056660)
XLA Ops:
  7.2 2.1 clamp_convert_fusion
  9.3 6.0 %stack.2 = bf16[8,128,8192]{2,1,0:T(8,128)(2,1)} broadcast(bf16[128,8192]{1,0:T(8,128)(2,1)S(1)} %clamp_convert_fusion), dimensions={1,2} | broadcast | bytes 18874368 | tf_op jit(solution)/shard_map/stack | solution.py:49
  15.3 0.0 copy-start
  15.3 0.0 copy-start.1
  15.3 5.9 %all-to-all-start = ((bf16[8,128,8192]{2,1,0:T(8,128)(2,1)}), bf16[8,128,8192]{2,1,0:T(8,128)(2,1)}, u32[]{:S(2)}, u32[]{:S(2)}) async-start(bf16[8,128,8192]{2,1,0:T(8,128)(2,1)} %stack.2), calls=%async_computation | async-start | bytes 33554432 | tf_op jit(solution)/shard_map/all_to_all | solution.py:49
  21.2 0.0 reduce-scatter.2.cloned.1.call-start
  22.0 0.3 broadcast_in_dim.25
  22.2 0.0 copy-done
  22.3 0.0 copy-done.1
  22.3 25.3 %while.15 = (s32[]{:T(128)}, bf16[1024,1024]{1,0:T(8,128)(2,1)S(1)}, bf16[1024,1024]{1,0:T(8,128)(2,1)}, bf16[1024,128]{1,0:T(8,128)(2,1)S(1)}, bf16[1024,128]{1...) while((s32[]{:T(128)}, bf16[1024,1024]{1,0:T(8,128)(2,1)S(1)}, ...), condition=%wide.region_3.4_spmd, body=%wide.region_0.3_spmd.sunk | while | flops 552990720 | bytes 13652127 | solution.py:43
  22.3 1.7 fusion.23
  24.0 0.5 fusion.24
  24.5 0.9 fusion.25
  25.4 1.7 fusion.23
  27.1 0.5 fusion.24
  27.6 0.9 fusion.25
  28.6 1.7 fusion.23
  30.3 0.5 fusion.24
  30.8 0.9 fusion.25
  31.8 1.7 fusion.23
  33.4 0.5 fusion.24
  34.0 0.9 fusion.25
  34.9 1.7 fusion.23
  36.6 0.5 fusion.24
  37.1 0.9 fusion.25
  38.1 1.7 fusion.23
  39.8 0.5 fusion.24
  40.3 0.9 fusion.25
  41.2 1.7 fusion.23
  42.9 0.5 fusion.24
  43.4 0.9 fusion.25
  44.4 1.7 fusion.23
  46.1 0.5 fusion.24
  46.6 0.9 fusion.25
  47.5 158.2 %all-to-all-done = bf16[8,128,8192]{2,1,0:T(8,128)(2,1)} async-done(((bf16[8,128,8192]{2,1,0:T(8,128)(2,1)}), bf16[8,128,8192]{2,1,0:T(8,128)(2,1)}, u32[]{:S(2)}, u32[]{:S(2)}) %all-to-all-start) | async-done | bytes 16777248 | tf_op jit(solution)/shard_map/all_to_all | solution.py:49
  205.8 27.4 %multiply_convert_fusion = bf16[8192,1024]{1,0:T(8,128)(2,1)} fusion(bf16[1024,8192]{1,0:T(8,128)(2,1)} %bitcast.1, bf16[1024,1024]{1,0:T(8,128)(2,1)S(1)} %get-tuple-element.158, f32[]{:T(128)} %bitcast.3), kind=kOutput, calls=%fused_computation.16 | convolution fusion | flops 17196646400 | bytes 35651588 | tf_op jit(solution)/shard_map/dot_general | solution.py:47
  233.1 0.0 reduce-scatter.2.cloned.1.call-update
  233.2 216.0 %reduce-scatter.2.cloned.1.call-done = bf16[512,1024]{1,0:T(8,128)(2,1)} async-done(((bf16[8192,1024]{1,0:T(8,128)(2,1)}), bf16[512,1024]{1,0:T(8,128)(2,1)}) %reduce-scatter.2.cloned.1.call-update) | async-done | bytes 1048592 | tf_op jit(solution)/shard_map/reduce_scatter | solution.py:56
  449.2 2.8 convert_element_type.54
Async XLA Ops:
  15.3 6.9 %copy-start = (bf16[1024,128]{1,0:T(8,128)(2,1)S(1)}, bf16[1024,128]{1,0:T(8,128)(2,1)}, u32[]{:S(2)}) copy-start(bf16[1024,128]{1,0:T(8,128)(2,1)} %param.9) | copy-start | bytes 786436
  15.3 7.0 %copy-start.1 = (bf16[1024,128]{1,0:T(8,128)(2,1)S(1)}, bf16[1024,128]{1,0:T(8,128)(2,1)}, u32[]{:S(2)}) copy-start(bf16[1024,128]{1,0:T(8,128)(2,1)} %param.10) | copy-start | bytes 786436
  15.3 190.4 %all-to-all-start = ((bf16[8,128,8192]{2,1,0:T(8,128)(2,1)}), bf16[8,128,8192]{2,1,0:T(8,128)(2,1)}, u32[]{:S(2)}, u32[]{:S(2)}) async-start(bf16[8,128,8192]{2,1,0:T(8,128)(2,1)} %stack.2), calls=%async_computation | async-start | bytes 33554432 | tf_op jit(solution)/shard_map/all_to_all | solution.py:49
  21.2 427.9 %reduce-scatter.2.cloned.1.call-start = ((), (), s32[]{:S(2)}) async-start(), calls=%async_computation.2 | async-start | bytes 17825792 | tf_op jit(solution)/shard_map/reduce_scatter | solution.py:56
Sparse Core Ops, SparseCore 0:
  233.3 215.8 reduce-scatter.1
